TPU v7x, 32 devices: a whole 2x2x4 slice. The times are simulated.
32 devices in a mesh: dp: 8 (over z, y), seq: 4 (over x, core).
Axes of the slice: x: 2, y: 2, z: 4, core: 2. Of those that a mesh axis runs over, the one named last changes fastest.
Arguments:
- queries: bfloat16 [8, 512, 2048], P('dp', 'seq'), may hold values from -5 to 5
- keys: bfloat16 [8, 512, 2048], P('dp', 'seq'), may hold values from -5 to 5
- values: bfloat16 [8, 512, 2048], P('dp', 'seq'), may hold values from -6 to 6
- stream: bfloat16 [8, 512, 2048], P('dp', 'seq'), may hold values from -40 to 40
- layer_scale: float32 [2048], replicated, may hold values from 0.5 to 2
- norm_gain: float32 [2048], replicated, may hold values from 0.5 to 2
- teacher_gram: bfloat16 [8, 512, 512], P('dp', 'seq'), may hold values from -20 to 20, as said below
Outputs:
- feature_grad: bfloat16 [8, 512, 2048], P('dp', 'seq')
- image_loss: float32 [8], P('dp')
- mean_loss: float32 [], replicated
Inputs may be any that keep to these rules, and one draw needn't show every extreme that they name: Each image's teacher_gram is symmetric.
All inputs are finite; a program needn't handle non-finite values.
Results may differ from a plain program's by a relative error of at most 0.009.
Values may be sent and summed in bfloat16 or wider, within the bound.
A program may use at most 64 MiB of HBM per device.

v0:
```python
import math
import jax
import jax.numpy as jnp
from jax import lax
from jax.sharding import PartitionSpec as P

HEAD_DIM = 64
EPSILON = 1e-06


def attend_block(q_block, k_head, v_head):
    scores = jnp.einsum(
        "qd,kd->qk", q_block, k_head, preferred_element_type=jnp.float32
    ) / math.sqrt(q_block.shape[1])
    row_max = jnp.max(scores, axis=1, keepdims=True)
    exponent = jnp.exp(scores - row_max)
    weights = (exponent / jnp.sum(exponent, axis=1, keepdims=True)).astype(jnp.bfloat16)
    return jnp.dot(weights, v_head, preferred_element_type=jnp.float32).astype(jnp.bfloat16)


def attend_head(q_head, k_head, v_head):
    row_count, head_depth = q_head.shape
    block_rows = math.gcd(row_count, 512)
    blocks = q_head.reshape(row_count // block_rows, block_rows, head_depth)
    results = lax.map(lambda q_block: attend_block(q_block, k_head, v_head), blocks)
    return results.reshape(row_count, head_depth)


def forward_norm(summed, norm_gain):
    row_mean = jnp.mean(summed, axis=-1, keepdims=True)
    centred = summed - row_mean
    variance = jnp.mean(centred * centred, axis=-1, keepdims=True)
    inv_sigma = lax.rsqrt(variance + EPSILON)
    centred_hat = centred * inv_sigma
    normed = centred_hat * norm_gain
    inv_length = lax.rsqrt(jnp.sum(normed * normed, axis=-1, keepdims=True) + EPSILON)
    return (centred_hat, inv_sigma, normed, inv_length)


def backward_norm(cotangent, centred_hat, inv_sigma, normed, inv_length, norm_gain):
    along = jnp.sum(normed * cotangent, axis=-1, keepdims=True)
    grad_normed = inv_length * cotangent - inv_length * inv_length * inv_length * normed * along
    scaled = grad_normed * norm_gain
    mean_scaled = jnp.mean(scaled, axis=-1, keepdims=True)
    mean_product = jnp.mean(scaled * centred_hat, axis=-1, keepdims=True)
    return (scaled - mean_scaled - centred_hat * mean_product) * inv_sigma


def local(queries, keys, values, stream, layer_scale, norm_gain, teacher_gram):
    head_q, head_k, head_v = (
        lax.all_to_all(queries[0], "seq", split_axis=1, concat_axis=0, tiled=True),
        lax.all_to_all(keys[0], "seq", split_axis=1, concat_axis=0, tiled=True),
        lax.all_to_all(values[0], "seq", split_axis=1, concat_axis=0, tiled=True),
    )
    head_count = head_q.shape[1] // HEAD_DIM
    pieces = []
    for head_index in range(head_count):
        low_col = head_index * HEAD_DIM
        high_col = low_col + HEAD_DIM
        pieces.append(
            attend_head(
                head_q[:, low_col:high_col],
                head_k[:, low_col:high_col],
                head_v[:, low_col:high_col],
            )
        )
    attended_heads = jnp.concatenate(pieces, axis=1)
    attended = lax.all_to_all(attended_heads, "seq", split_axis=0, concat_axis=1, tiled=True)
    summed = stream[0].astype(jnp.float32) + layer_scale * attended.astype(jnp.float32)
    centred_hat, inv_sigma, normed, inv_length = forward_norm(summed, norm_gain)
    features = (normed * inv_length).astype(jnp.bfloat16)
    teacher_rows = teacher_gram[0]
    row_count, width_all = features.shape
    cycle_size = lax.axis_size("seq")
    tokens_all = row_count * cycle_size
    piece = lax.all_gather(features, "seq", axis=0, tiled=True)
    gram_tile = jnp.einsum("ad,bd->ab", features, piece, preferred_element_type=jnp.float32)
    taught = teacher_rows.astype(jnp.float32)
    differ = gram_tile - taught
    grad_acc = jnp.dot(differ.astype(jnp.bfloat16), piece, preferred_element_type=jnp.float32)
    loss_part = jnp.sum(differ * differ)
    loss_weight = width_all / (tokens_all * tokens_all)
    cotangent = grad_acc * (4.0 * width_all / (tokens_all * tokens_all))
    grad_summed = backward_norm(cotangent, centred_hat, inv_sigma, normed, inv_length, norm_gain)
    feature_grad = (grad_summed * (tokens_all * math.sqrt(width_all))).astype(jnp.bfloat16)[None]
    image_count = lax.axis_size("dp")
    image_total = lax.psum(loss_part, "seq")
    image_loss = image_total * loss_weight
    mean_loss = lax.psum(image_loss, "dp") / image_count
    return (feature_grad, jnp.reshape(image_loss, (1,)), mean_loss)


def solution(mesh):
    return jax.shard_map(
        local,
        mesh=mesh,
        in_specs=(
            P("dp", "seq", None),
            P("dp", "seq", None),
            P("dp", "seq", None),
            P("dp", "seq", None),
            P(),
            P(),
            P("dp", "seq", None),
        ),
        out_specs=(P("dp", "seq", None), P("dp"), P()),
        check_vma=False,
    )
```

profile of v0, /device:TPU:0, one launch (start us, length us, event | category | flops | bytes accessed | tf_op | source)
XLA Modules:
  0.0 143.6 jit_solution(15839510639580892488)
XLA Ops:
  7.2 2.1 %copy.19 = bf16[1,128,2048]{1,2,0:T(8,128)(2,1)} copy(bf16[1,128,2048]{2,1,0:T(8,128)(2,1)} %param.7) | data formatting | bytes 1048576 | tf_op args[0]
  9.3 4.2 %all-to-all-start = ((bf16[128,4,512]{0,2,1:T(8,128)(2,1)}), bf16[128,4,512]{0,2,1:T(8,128)(2,1)S(1)}, u32[]{:S(2)}, u32[]{:S(2)}) async-start(bf16[128,4,512]{0,2,1:T(8,128)(2,1)} %bitcast.1), calls=%async_computation | async-start | bytes 1048576 | tf_op jit(solution)/shard_map/all_to_all | solution.py:51
  13.5 1.0 copy.21
  14.5 7.8 %all-to-all-done = bf16[128,4,512]{0,2,1:T(8,128)(2,1)S(1)} async-done(((bf16[128,4,512]{0,2,1:T(8,128)(2,1)}), bf16[128,4,512]{0,2,1:T(8,128)(2,1)S(1)}, u32[]{:S(2)}, u32[]{:S(2)}) %all-to-all-start) | async-done | bytes 524320 | tf_op jit(solution)/shard_map/all_to_all | solution.py:51
  22.4 3.5 %all-to-all-start.1 = ((bf16[128,4,512]{0,2,1:T(8,128)(2,1)}), bf16[128,4,512]{0,2,1:T(8,128)(2,1)S(1)}, u32[]{:S(2)}, u32[]{:S(2)}) async-start(bf16[128,4,512]{0,2,1:T(8,128)(2,1)} %bitcast.4), calls=%async_computation.1 | async-start | bytes 1048576 | tf_op jit(solution)/shard_map/all_to_all | solution.py:52
  25.8 1.0 copy.23
  27.1 7.5 %all-to-all-done.1 = bf16[128,4,512]{0,2,1:T(8,128)(2,1)S(1)} async-done(((bf16[128,4,512]{0,2,1:T(8,128)(2,1)}), bf16[128,4,512]{0,2,1:T(8,128)(2,1)S(1)}, u32[]{:S(2)}, u32[]{:S(2)}) %all-to-all-start.1) | async-done | bytes 524320 | tf_op jit(solution)/shard_map/all_to_all | solution.py:52
  34.6 4.1 %all-to-all-start.2 = ((bf16[128,4,512]{0,2,1:T(8,128)(2,1)}), bf16[128,4,512]{0,2,1:T(8,128)(2,1)}, u32[]{:S(2)}, u32[]{:S(2)}) async-start(bf16[128,4,512]{0,2,1:T(8,128)(2,1)} %bitcast.7), calls=%async_computation.2 | async-start | bytes 1048576 | tf_op jit(solution)/shard_map/all_to_all | solution.py:53
  39.0 1.4 fusion.46
  40.4 1.3 fusion.45
  41.7 1.3 fusion.47
  43.0 1.4 fusion.48
  44.4 1.3 fusion.49
  45.6 1.4 fusion.50
  47.4 0.4 fusion.52
  47.8 1.2 copy.24
  49.0 1.4 fusion.9
  50.4 1.6 %fusion.1 = bf16[8,4,8,128]{3,2,1,0:T(8,128)(2,1)S(1)} fusion(f32[512,512]{0,1:T(8,128)} %get-tuple-element.103, f32[512]{0:T(512)S(1)} %fusion.9, f32[512]{0:T(512)S(1)} %get-tuple-element.102, bf16[512,512]{1,0:T(8,128)(2,1)S(1)} %bitcast.83), kind=kOutput, calls=%fused_computation.18 | convolution fusion | flops 34373632 | bytes 1249280 | tf_op jit(solution)/shard_map/while/body/eval_jaxpr/dot_general | solution.py:18
  52.6 0.9 copy-done.5
  54.0 0.9 copy-done.4
  55.5 0.9 copy-done.3
  56.9 0.9 copy-done.2
  59.5 11.8 %all_to_all.67 = bf16[4,128,512]{1,2,0:T(8,128)(2,1)S(1)} all-to-all(bf16[4,128,512]{1,2,0:T(8,128)(2,1)S(1)} %bitcast_dynamic-update-slice_fusion), channel_id=1, replica_groups=mesh['dp'=8,'seq'=4] {'seq'}, dimensions={0} | all-to-all | bytes 1048576 | tf_op jit(solution)/shard_map/all_to_all | solution.py:68
  71.8 0.6 copy-done.1
  73.5 0.9 multiply_convert_fusion.1
  74.5 23.7 %all-gather.2.cloned.1.call-done = bf16[512,2048]{1,0:T(8,128)(2,1)} async-done(((bf16[128,2048]{1,0:T(8,128)(2,1)}), bf16[512,2048]{1,0:T(8,128)(2,1)}) %all-gather.2.cloned.1.call-update) | async-done | bytes 2097168 | tf_op jit(solution)/shard_map/all_gather | solution.py:76
  98.2 3.4 %multiply_reduce_fusion.4 = (f32[]{:T(128)}, bf16[128,512]{1,0:T(8,128)(2,1)S(1)}) fusion(bf16[1,128,512]{2,1,0:T(8,128)(2,1)S(1)} %copy-done.10, bf16[128,2048]{1,0:T(8,128)(2,1)} %multiply_convert_fusion.1, bf16[512,2048]{1,0:T(8,128)(2,1)} %all-gather.2.cloned.1.call-done), kind=kOutput, calls=%fused_computation.60 | convolution fusion | flops 268763136 | bytes 2883588 | tf_op jit(solution)/shard_map/ad,bd->ab/dot_general | solution.py:77
  101.6 6.5 %psum.14 = f32[]{:T(128)} all-reduce(f32[]{:T(128)} %get-tuple-element.133), channel_id=1, replica_groups=mesh['dp'=8,'seq'=4] {'seq'}, use_global_device_ids=true, to_apply=%region_23.24 | all-reduce | flops 1 | bytes 8 | tf_op jit(solution)/shard_map/psum | solution.py:87
  108.7 22.7 %psum.15 = f32[]{:T(128)} all-reduce(f32[]{:T(128)} %mul.157), channel_id=1, replica_groups=mesh['dp'=8,'seq'=4] {'dp'}, use_global_device_ids=true, to_apply=%region_24.25 | all-reduce | flops 1 | bytes 8 | tf_op jit(solution)/shard_map/psum | solution.py:89
  131.4 0.6 multiply_reduce_fusion.1
  132.0 0.5 fusion.44
  132.5 1.4 fusion.16
  (56 shorter events, 6.1 us)
Async XLA Ops:
  7.2 6.4 %copy-start.7 = (bf16[1,128,2048]{2,1,0:T(8,128)(2,1)S(1)}, bf16[1,128,2048]{2,1,0:T(8,128)(2,1)}, u32[]{:S(2)}) copy-start(bf16[1,128,2048]{2,1,0:T(8,128)(2,1)} %param.8) | copy-start | bytes 1572868
  7.2 18.7 %copy-start.8 = (bf16[1,128,2048]{2,1,0:T(8,128)(2,1)S(1)}, bf16[1,128,2048]{2,1,0:T(8,128)(2,1)}, u32[]{:S(2)}) copy-start(bf16[1,128,2048]{2,1,0:T(8,128)(2,1)} %param.9) | copy-start | bytes 1572868
  9.3 13.1 %all-to-all-start = ((bf16[128,4,512]{0,2,1:T(8,128)(2,1)}), bf16[128,4,512]{0,2,1:T(8,128)(2,1)S(1)}, u32[]{:S(2)}, u32[]{:S(2)}) async-start(bf16[128,4,512]{0,2,1:T(8,128)(2,1)} %bitcast.1), calls=%async_computation | async-start | bytes 1048576 | tf_op jit(solution)/shard_map/all_to_all | solution.py:51
  22.4 12.3 %all-to-all-start.1 = ((bf16[128,4,512]{0,2,1:T(8,128)(2,1)}), bf16[128,4,512]{0,2,1:T(8,128)(2,1)S(1)}, u32[]{:S(2)}, u32[]{:S(2)}) async-start(bf16[128,4,512]{0,2,1:T(8,128)(2,1)} %bitcast.4), calls=%async_computation.1 | async-start | bytes 1048576 | tf_op jit(solution)/shard_map/all_to_all | solution.py:52
  34.6 13.1 %all-to-all-start.2 = ((bf16[128,4,512]{0,2,1:T(8,128)(2,1)}), bf16[128,4,512]{0,2,1:T(8,128)(2,1)}, u32[]{:S(2)}, u32[]{:S(2)}) async-start(bf16[128,4,512]{0,2,1:T(8,128)(2,1)} %bitcast.7), calls=%async_computation.2 | async-start | bytes 1048576 | tf_op jit(solution)/shard_map/all_to_all | solution.py:53
  38.8 59.4 %all-gather.2.cloned.1.call-start = ((), (), s32[]{:S(2)}) async-start(), calls=%async_computation.4 | async-start | bytes 2621440 | tf_op jit(solution)/shard_map/all_gather | solution.py:76
  50.4 1.7 %copy-start.6 = (f32[512,512]{0,1:T(8,128)S(1)}, f32[512,512]{0,1:T(8,128)}, u32[]{:S(2)}) copy-start(f32[512,512]{0,1:T(8,128)} %get-tuple-element.101) | copy-start | bytes 3145732
  52.3 1.2 copy-start.5
  53.7 1.2 copy-start.4
  55.1 1.2 copy-start.3
  56.5 1.2 copy-start.2
  71.4 1.0 copy-start.1
  71.4 1.0 copy-start.11
  72.4 0.7 copy-start.9
  73.1 25.1 %copy-start.10 = (bf16[1,128,512]{2,1,0:T(8,128)(2,1)S(1)}, bf16[1,128,512]{2,1,0:T(8,128)(2,1)}, u32[]{:S(2)}) copy-start(bf16[1,128,512]{2,1,0:T(8,128)(2,1)} %param.13) | copy-start | bytes 393220
  98.2 33.2 %copy-start = (bf16[512,2048]{1,0:T(8,128)(2,1)S(1)}, bf16[512,2048]{1,0:T(8,128)(2,1)}, u32[]{:S(2)}) copy-start(bf16[512,2048]{1,0:T(8,128)(2,1)} %all-gather.2.cloned.1.call-done) | copy-start | bytes 6291460
Sparse Core Ops, SparseCore 0:
  74.6 23.5 all-gather.1
where the time goes:
time: 144 us
  blocking collectives  41 us (28%)
  waiting for transfers between devices  39.1 us (27%)
  between operations  17.8 us (12%)
  matrix products  16.5 us (11%)
  starting transfers between devices  11.9 us (8%)
  local copies, waits for them, and re-layouts  10.7 us (7%)
  other arithmetic  6.59 us (5%)
    all_gather x1, waiting for transfers between devices, local(): piece = lax.all_gather(features, 'seq', axis=0, tiled=True)  23.7 us
    psum x1, blocking collectives, local(): mean_loss = lax.psum(image_loss, 'dp') / image_count  22.7 us
    all_to_all x1, blocking collectives, local(): lax.all_to_all(attended_heads, 'seq', split_axis=0, concat_axis=1, tiled=...  11.8 us
    dot_general x8, matrix products, attend_block(): jnp.einsum('qd,kd->qk', q_block, k_head, preferred_element_type=jnp.float32)  8.71 us
    unnamed x34, local copies, waits for them, and re-layouts  8.69 us
    all_to_all x1, waiting for transfers between devices, local(): lax.all_to_all(queries[0], 'seq', split_axis=1, concat_axis=0, tiled=True)  7.81 us
    all_to_all x1, waiting for transfers between devices, local(): lax.all_to_all(keys[0], 'seq', split_axis=1, concat_axis=0, tiled=True)  7.52 us
    psum x1, blocking collectives, local(): image_total = lax.psum(loss_part, 'seq')  6.49 us
  transfers between devices with their start and end apart: 4, of which 3 were waited for; matrix products, arithmetic and copies ran while one was open for 8% of the time, Pallas kernels for 0%

commit v1 on v0

--- a/solution.py
+++ b/solution.py
@@ -73,7 +73,12 @@
     row_count, width_all = features.shape
     cycle_size = lax.axis_size("seq")
     tokens_all = row_count * cycle_size
-    piece = lax.all_gather(features, "seq", axis=0, tiled=True)
+    ring = [features]
+    for hop in range(3):
+        ring.append(lax.ppermute(ring[-1], "seq", [(dev, (dev + 1) % 4) for dev in range(4)]))
+    piece = jnp.roll(
+        jnp.concatenate(ring[::-1], axis=0), (lax.axis_index("seq") + 1) * ring[0].shape[0], axis=0
+    )
     gram_tile = jnp.einsum("ad,bd->ab", features, piece, preferred_element_type=jnp.float32)
     taught = teacher_rows.astype(jnp.float32)
     differ = gram_tile - taught

time: 144 us -> 132 us (0.917)
  between operations: 17.8 us -> 4.54 us
    ppermute x0 -> x3, waiting for transfers between devices: none -> 25.8 us  [local(): lax.ppermute(ring[-1], 'seq', [(dev, (dev + 1) % 4) for dev in range(4)])]
    all_gather x1 -> x0, waiting for transfers between devices: 23.7 us -> none  [local(): piece = lax.all_gather(features, 'seq', axis=0, tiled=True)]
    dot_general x1, matrix products: 3.37 us -> 1.5 us  [local(): jnp.einsum('ad,bd->ab', features, piece, preferred_element_type=jnp.float32)]
    dot_general x1, matrix products: 0.56 us -> 2.16 us  [local(): jnp.dot(differ.astype(jnp.bfloat16), piece, preferred_element_type=jnp.fl...]
    unnamed x34 -> x40, local copies, waits for them, and re-layouts: 8.69 us -> 8.28 us
  transfers between devices with their start and end apart: 4 -> 6, of which waited for: 3 -> 5; matrix products, arithmetic and copies ran while one was open for 8% -> 9% of each run, Pallas kernels for 0% -> 0%
where the time goes in v1:
time: 132 us
  blocking collectives  41.8 us (32%)
  waiting for transfers between devices  40.1 us (30%)
  matrix products  16.3 us (12%)
  starting transfers between devices  11.9 us (9%)
  local copies, waits for them, and re-layouts  11.2 us (8%)
  other arithmetic  6.03 us (5%)
  between operations  4.54 us (3%)
    ppermute x3, waiting for transfers between devices, local(): lax.ppermute(ring[-1], 'seq', [(dev, (dev + 1) % 4) for dev in range(4)])  25.8 us
    psum x1, blocking collectives, local(): mean_loss = lax.psum(image_loss, 'dp') / image_count  23.6 us
    all_to_all x1, blocking collectives, local(): lax.all_to_all(attended_heads, 'seq', split_axis=0, concat_axis=1, tiled=...  11.9 us
    dot_general x8, matrix products, attend_block(): jnp.einsum('qd,kd->qk', q_block, k_head, preferred_element_type=jnp.float32)  8.72 us
    unnamed x40, local copies, waits for them, and re-layouts  8.28 us
    all_to_all x1, waiting for transfers between devices, local(): lax.all_to_all(keys[0], 'seq', split_axis=1, concat_axis=0, tiled=True)  7.52 us
    all_to_all x1, waiting for transfers between devices, local(): lax.all_to_all(queries[0], 'seq', split_axis=1, concat_axis=0, tiled=True)  6.77 us
    psum x1, blocking collectives, local(): image_total = lax.psum(loss_part, 'seq')  6.37 us
  transfers between devices with their start and end apart: 6, of which 5 were waited for; matrix products, arithmetic and copies ran while one was open for 9% of the time, Pallas kernels for 0%

profile of v1, /device:TPU:0, one launch (start us, length us, event | category | flops | bytes accessed | tf_op | source)
XLA Modules:
  0.0 131.8 jit_solution(5654215538574417387)
XLA Ops:
  0.6 2.1 %copy.19 = bf16[1,128,2048]{1,2,0:T(8,128)(2,1)} copy(bf16[1,128,2048]{2,1,0:T(8,128)(2,1)} %param.7) | data formatting | bytes 1048576 | tf_op args[0]
  2.7 4.2 %all-to-all-start = ((bf16[128,4,512]{0,2,1:T(8,128)(2,1)}), bf16[128,4,512]{0,2,1:T(8,128)(2,1)S(1)}, u32[]{:S(2)}, u32[]{:S(2)}) async-start(bf16[128,4,512]{0,2,1:T(8,128)(2,1)} %bitcast.1), calls=%async_computation | async-start | bytes 1048576 | tf_op jit(solution)/shard_map/all_to_all | solution.py:51
  7.0 2.0 %copy.21 = bf16[1,128,2048]{1,2,0:T(8,128)(2,1)} copy(bf16[1,128,2048]{2,1,0:T(8,128)(2,1)} %param.8) | data formatting | bytes 1048576 | tf_op args[1]
  9.0 6.8 %all-to-all-done = bf16[128,4,512]{0,2,1:T(8,128)(2,1)S(1)} async-done(((bf16[128,4,512]{0,2,1:T(8,128)(2,1)}), bf16[128,4,512]{0,2,1:T(8,128)(2,1)S(1)}, u32[]{:S(2)}, u32[]{:S(2)}) %all-to-all-start) | async-done | bytes 524320 | tf_op jit(solution)/shard_map/all_to_all | solution.py:51
  15.8 3.5 %all-to-all-start.1 = ((bf16[128,4,512]{0,2,1:T(8,128)(2,1)}), bf16[128,4,512]{0,2,1:T(8,128)(2,1)S(1)}, u32[]{:S(2)}, u32[]{:S(2)}) async-start(bf16[128,4,512]{0,2,1:T(8,128)(2,1)} %bitcast.4), calls=%async_computation.1 | async-start | bytes 1048576 | tf_op jit(solution)/shard_map/all_to_all | solution.py:52
  19.3 1.0 copy.23
  20.5 7.5 %all-to-all-done.1 = bf16[128,4,512]{0,2,1:T(8,128)(2,1)S(1)} async-done(((bf16[128,4,512]{0,2,1:T(8,128)(2,1)}), bf16[128,4,512]{0,2,1:T(8,128)(2,1)S(1)}, u32[]{:S(2)}, u32[]{:S(2)}) %all-to-all-start.1) | async-done | bytes 524320 | tf_op jit(solution)/shard_map/all_to_all | solution.py:52
  28.0 4.1 %all-to-all-start.2 = ((bf16[128,4,512]{0,2,1:T(8,128)(2,1)}), bf16[128,4,512]{0,2,1:T(8,128)(2,1)}, u32[]{:S(2)}, u32[]{:S(2)}) async-start(bf16[128,4,512]{0,2,1:T(8,128)(2,1)} %bitcast.7), calls=%async_computation.2 | async-start | bytes 1048576 | tf_op jit(solution)/shard_map/all_to_all | solution.py:53
  32.4 1.4 %fusion.54 = (f32[512]{0:T(512)S(1)}, f32[512,512]{0,1:T(8,128)}) fusion(bf16[512,512]{1,0:T(8,128)(2,1)S(1)} %bitcast.70, bf16[512,512]{1,0:T(8,128)(2,1)S(1)} %bitcast.62), kind=kOutput, calls=%fused_computation.117 | convolution fusion | flops 34078208 | bytes 1312768 | tf_op jit(solution)/shard_map/while/body/eval_jaxpr/qd,kd->qk/dot_general | solution.py:12
  33.8 1.3 fusion.53
  35.1 1.3 fusion.55
  36.4 1.4 %fusion.56 = (f32[512]{0:T(512)S(1)}, f32[512,512]{0,1:T(8,128)}) fusion(bf16[512,512]{1,0:T(8,128)(2,1)S(1)} %bitcast.73, bf16[512,512]{1,0:T(8,128)(2,1)S(1)} %bitcast.65), kind=kOutput, calls=%fused_computation.119 | convolution fusion | flops 34078208 | bytes 1312768 | tf_op jit(solution)/shard_map/while/body/eval_jaxpr/qd,kd->qk/dot_general | solution.py:12
  37.8 1.3 fusion.57
  39.0 1.4 %fusion.58 = (f32[512]{0:T(512)S(1)}, f32[512,512]{0,1:T(8,128)}) fusion(bf16[512,512]{1,0:T(8,128)(2,1)S(1)} %bitcast.75, bf16[512,512]{1,0:T(8,128)(2,1)S(1)} %bitcast.67), kind=kOutput, calls=%fused_computation.121 | convolution fusion | flops 34078208 | bytes 1312768 | tf_op jit(solution)/shard_map/while/body/eval_jaxpr/qd,kd->qk/dot_general | solution.py:12
  40.7 0.4 fusion.60
  41.2 2.1 %copy.24 = bf16[4,128,512]{2,1,0:T(8,128)(2,1)} copy(bf16[4,128,512]{1,2,0:T(8,128)(2,1)} %bitcast.8) | data formatting | bytes 1048576 | tf_op jit(solution)/shard_map/all_to_all | solution.py:53
  43.3 1.5 %fusion.16 = f32[512]{0:T(512)S(1)} fusion(f32[512,512]{0,1:T(8,128)} %get-tuple-element.103, f32[512]{0:T(512)S(1)} %get-tuple-element.102), kind=kLoop, calls=%fused_computation.55 | loop fusion | flops 523776 | bytes 1052672 | tf_op jit(solution)/shard_map/while/body/eval_jaxpr/reduce_sum | solution.py:17
  44.8 1.6 %fusion.8 = bf16[8,4,8,128]{3,2,1,0:T(8,128)(2,1)S(1)} fusion(f32[512,512]{0,1:T(8,128)} %get-tuple-element.103, f32[512]{0:T(512)S(1)} %fusion.16, f32[512]{0:T(512)S(1)} %get-tuple-element.102, bf16[512,512]{1,0:T(8,128)(2,1)} %bitcast.81), kind=kOutput, calls=%fused_computation.22 | convolution fusion | flops 34373632 | bytes 1249280 | tf_op jit(solution)/shard_map/while/body/eval_jaxpr/dot_general | solution.py:18
  47.5 0.4 copy-done.4
  49.0 0.4 copy-done.2
  51.1 11.9 %all_to_all.67 = bf16[4,128,512]{1,2,0:T(8,128)(2,1)S(1)} all-to-all(bf16[4,128,512]{1,2,0:T(8,128)(2,1)S(1)} %bitcast_dynamic-update-slice_fusion), channel_id=1, replica_groups=mesh['dp'=8,'seq'=4] {'seq'}, dimensions={0} | all-to-all | bytes 1048576 | tf_op jit(solution)/shard_map/all_to_all | solution.py:68
  64.0 0.4 multiply_reduce_fusion.2
  64.6 8.6 %collective-permute-done = bf16[128,2048]{1,0:T(8,128)(2,1)S(1)} collective-permute-done((bf16[128,2048]{1,0:T(8,128)(2,1)S(1)}, bf16[128,2048]{1,0:T(8,128)(2,1)S(1)}, u32[]{:S(2)}, u32[]{:S(2)}) %collective-permute-start) | collective-permute-done | bytes 524320 | tf_op jit(solution)/shard_map/ppermute | solution.py:78
  73.2 8.6 %collective-permute-done.1 = bf16[128,2048]{1,0:T(8,128)(2,1)S(1)} collective-permute-done((bf16[128,2048]{1,0:T(8,128)(2,1)S(1)}, bf16[128,2048]{1,0:T(8,128)(2,1)S(1)}, u32[]{:S(2)}, u32[]{:S(2)}) %collective-permute-start.1) | collective-permute-done | bytes 524320 | tf_op jit(solution)/shard_map/ppermute | solution.py:78
  81.8 8.6 %collective-permute-done.2 = bf16[128,2048]{1,0:T(8,128)(2,1)S(1)} collective-permute-done((bf16[128,2048]{1,0:T(8,128)(2,1)S(1)}, bf16[128,2048]{1,0:T(8,128)(2,1)S(1)}, u32[]{:S(2)}, u32[]{:S(2)}) %collective-permute-start.2) | collective-permute-done | bytes 524320 | tf_op jit(solution)/shard_map/ppermute | solution.py:78
  90.9 1.9 %copy-done = bf16[1024,2048]{1,0:T(8,128)(2,1)} copy-done((bf16[1024,2048]{1,0:T(8,128)(2,1)}, bf16[1024,2048]{1,0:T(8,128)(2,1)S(1)}, u32[]{:S(2)}) %copy-start) | copy-done | bytes 4194328
  92.8 1.5 %multiply_reduce_fusion.4 = (f32[]{:T(128)}, bf16[128,512]{1,0:T(8,128)(2,1)S(1)}) fusion(bf16[1,128,512]{2,1,0:T(8,128)(2,1)S(1)} %copy-done.10, bf16[128,2048]{1,0:T(8,128)(2,1)S(1)} %multiply_convert_fusion.1, bf16[1024,2048]{1,0:T(8,128)(2,1)S(1)} %constant_dynamic-update-slice_fusion, s32[]{:T(128)S(6)} %select_n.14), kind=kOutput, calls=%fused_computation.64 | convolution fusion | flops 268763136 | bytes 2883592 | tf_op jit(solution)/shard_map/ad,bd->ab/dot_general | solution.py:82
  94.3 6.4 %psum.14 = f32[]{:T(128)} all-reduce(f32[]{:T(128)} %get-tuple-element.133), channel_id=1, replica_groups=mesh['dp'=8,'seq'=4] {'seq'}, use_global_device_ids=true, to_apply=%region_23.24 | all-reduce | flops 1 | bytes 8 | tf_op jit(solution)/shard_map/psum | solution.py:92
  101.4 2.2 %multiply_reduce_fusion.1 = (f32[128]{0:T(128)S(1)}, f32[128,2048]{1,0:T(8,128)S(1)}) fusion(f32[128,2048]{1,0:T(8,128)S(1)} %get-tuple-element.91, f32[2048]{0:T(1024)S(1)} %copy-done.9, bf16[1024,2048]{1,0:T(8,128)(2,1)} %copy-done, s32[]{:T(128)S(6)} %select_n.14, bf16[128,512]{1,0:T(8,128)(2,1)S(1)} %get-tuple-element.134), kind=kOutput, calls=%fused_computation.33 | convolution fusion | flops 269483904 | bytes 4334084 | tf_op jit(solution)/shard_map/dot_general | solution.py:85
  103.5 23.6 %psum.15 = f32[]{:T(128)} all-reduce(f32[]{:T(128)} %mul.161), channel_id=1, replica_groups=mesh['dp'=8,'seq'=4] {'dp'}, use_global_device_ids=true, to_apply=%region_24.25 | all-reduce | flops 1 | bytes 8 | tf_op jit(solution)/shard_map/psum | solution.py:94
  127.1 0.4 fusion.52
  127.6 1.4 %fusion.23 = bf16[1,128,2048]{2,1,0:T(8,128)(2,1)} fusion(f32[128,2048]{1,0:T(8,128)S(1)} %get-tuple-element.91, f32[128]{0:T(128)S(1)} %get-tuple-element.140, f32[128]{0:T(128)S(1)} %get-tuple-element.141, f32[128]{0:T(128)S(1)} %add_rsqrt_fusion.1, f32[128]{0:T(128)S(1)} %get-tuple-element.131, f32[2048]{0:T(1024)S(1)} %copy-done.9, ...), kind=kLoop, calls=%fused_computation.62 | loop fusion | flops 3145728 | bytes 2632704 | tf_op jit(solution)/shard_map/broadcast_in_dim | solution.py:90
  (67 shorter events, 6.3 us)
Async XLA Ops:
  0.6 18.6 %copy-start.7 = (bf16[1,128,2048]{2,1,0:T(8,128)(2,1)S(1)}, bf16[1,128,2048]{2,1,0:T(8,128)(2,1)}, u32[]{:S(2)}) copy-start(bf16[1,128,2048]{2,1,0:T(8,128)(2,1)} %param.9) | copy-start | bytes 1572868
  2.7 13.1 %all-to-all-start = ((bf16[128,4,512]{0,2,1:T(8,128)(2,1)}), bf16[128,4,512]{0,2,1:T(8,128)(2,1)S(1)}, u32[]{:S(2)}, u32[]{:S(2)}) async-start(bf16[128,4,512]{0,2,1:T(8,128)(2,1)} %bitcast.1), calls=%async_computation | async-start | bytes 1048576 | tf_op jit(solution)/shard_map/all_to_all | solution.py:51
  15.8 12.3 %all-to-all-start.1 = ((bf16[128,4,512]{0,2,1:T(8,128)(2,1)}), bf16[128,4,512]{0,2,1:T(8,128)(2,1)S(1)}, u32[]{:S(2)}, u32[]{:S(2)}) async-start(bf16[128,4,512]{0,2,1:T(8,128)(2,1)} %bitcast.4), calls=%async_computation.1 | async-start | bytes 1048576 | tf_op jit(solution)/shard_map/all_to_all | solution.py:52
  28.0 13.1 %all-to-all-start.2 = ((bf16[128,4,512]{0,2,1:T(8,128)(2,1)}), bf16[128,4,512]{0,2,1:T(8,128)(2,1)}, u32[]{:S(2)}, u32[]{:S(2)}) async-start(bf16[128,4,512]{0,2,1:T(8,128)(2,1)} %bitcast.7), calls=%async_computation.2 | async-start | bytes 1048576 | tf_op jit(solution)/shard_map/all_to_all | solution.py:53
  41.1 5.3 %copy-start.6 = (f32[512,512]{0,1:T(8,128)S(1)}, f32[512,512]{0,1:T(8,128)}, u32[]{:S(2)}) copy-start(f32[512,512]{0,1:T(8,128)} %get-tuple-element.101) | copy-start | bytes 3145732
  43.3 3.3 %copy-start.8 = (bf16[4,128,512]{2,1,0:T(8,128)(2,1)S(1)}, bf16[4,128,512]{2,1,0:T(8,128)(2,1)}, u32[]{:S(2)}) copy-start(bf16[4,128,512]{2,1,0:T(8,128)(2,1)} %copy.24) | copy-start | bytes 1572868
  44.8 2.2 %copy-start.5 = (f32[512,512]{0,1:T(8,128)S(1)}, f32[512,512]{0,1:T(8,128)}, u32[]{:S(2)}) copy-start(f32[512,512]{0,1:T(8,128)} %get-tuple-element.110) | copy-start | bytes 3145732
  46.6 1.2 copy-start.4
  47.2 1.3 copy-start.3
  48.0 1.3 copy-start.2
  50.6 12.8 %copy-start.1 = (bf16[1,128,2048]{2,1,0:T(8,128)(2,1)S(1)}, bf16[1,128,2048]{2,1,0:T(8,128)(2,1)}, u32[]{:S(2)}) copy-start(bf16[1,128,2048]{2,1,0:T(8,128)(2,1)} %param.10) | copy-start | bytes 1572868
  50.6 12.8 %copy-start.11 = (f32[2048]{0:T(1024)S(1)}, f32[2048]{0:T(1024)}, u32[]{:S(2)}) copy-start(f32[2048]{0:T(1024)} %param.11) | copy-start | bytes 24580
  51.0 12.9 %copy-start.9 = (f32[2048]{0:T(1024)S(1)}, f32[2048]{0:T(1024)}, u32[]{:S(2)}) copy-start(f32[2048]{0:T(1024)} %param.12) | copy-start | bytes 24580
  64.5 8.7 %collective-permute-start = (bf16[128,2048]{1,0:T(8,128)(2,1)S(1)}, bf16[128,2048]{1,0:T(8,128)(2,1)S(1)}, u32[]{:S(2)}, u32[]{:S(2)}) collective-permute-start(bf16[128,2048]{1,0:T(8,128)(2,1)S(1)} %multiply_convert_fusion.1), channel_id=1, source_target_pairs={{0,1},{1,2},{2,3},{3,0},{4,5},{5,6},{6,7},{7,4},{8,9},{9,10},{10,1... | collective-permute-start | bytes 1572872 | tf_op jit(solution)/shard_map/ppermute | solution.py:78
  73.2 8.6 %collective-permute-start.1 = (bf16[128,2048]{1,0:T(8,128)(2,1)S(1)}, bf16[128,2048]{1,0:T(8,128)(2,1)S(1)}, u32[]{:S(2)}, u32[]{:S(2)}) collective-permute-start(bf16[128,2048]{1,0:T(8,128)(2,1)S(1)} %collective-permute-done), channel_id=1, source_target_pairs={{0,1},{1,2},{2,3},{3,0},{4,5},{5,6},{6,7},{7,4},{8,9},{9,10},{10,1... | collective-permute-start | bytes 1572872 | tf_op jit(solution)/shard_map/ppermute | solution.py:78
  81.8 8.6 %collective-permute-start.2 = (bf16[128,2048]{1,0:T(8,128)(2,1)S(1)}, bf16[128,2048]{1,0:T(8,128)(2,1)S(1)}, u32[]{:S(2)}, u32[]{:S(2)}) collective-permute-start(bf16[128,2048]{1,0:T(8,128)(2,1)S(1)} %collective-permute-done.1), channel_id=1, source_target_pairs={{0,1},{1,2},{2,3},{3,0},{4,5},{5,6},{6,7},{7,4},{8,9},{9,10},{10,1... | collective-permute-start | bytes 1572872 | tf_op jit(solution)/shard_map/ppermute | solution.py:78
  90.4 2.4 %copy-start.10 = (bf16[1,128,512]{2,1,0:T(8,128)(2,1)S(1)}, bf16[1,128,512]{2,1,0:T(8,128)(2,1)}, u32[]{:S(2)}) copy-start(bf16[1,128,512]{2,1,0:T(8,128)(2,1)} %param.13) | copy-start | bytes 393220
  90.9 1.9 %copy-start = (bf16[1024,2048]{1,0:T(8,128)(2,1)}, bf16[1024,2048]{1,0:T(8,128)(2,1)S(1)}, u32[]{:S(2)}) copy-start(bf16[1024,2048]{1,0:T(8,128)(2,1)S(1)} %constant_dynamic-update-slice_fusion) | copy-start | bytes 12582916
